TPU v7x, 32 devices: a whole 2x2x4 slice. The times are simulated.
32 devices in a mesh: groups: 2 (over y), vel: 4 (over z), space: 2 (over x), spec: 2 (over core).
Axes of the slice: x: 2, y: 2, z: 4, core: 2. Of those that a mesh axis runs over, the one named last changes fastest.
Arguments:
- distribution: float32 [2, 32, 64, 32768], P('spec', ('groups', 'space'), None, 'vel'), parts along dimension 1, may hold values from 0.25 to 4
- vel_order: int32 [32768], P('vel'), may hold values from 0 to 32767, each once
- species_mass: int32 [2], P('spec'), may hold values from 1 to 8
- wall_mask: int32 [32, 2], P(('groups', 'space')), parts along dimension 0, may hold values 0 or 1
- inflow_mask: int32 [32, 2], P(('groups', 'space')), parts along dimension 0, may hold values 0 or 1
Outputs:
- updated: float32 [2, 32, 64, 32768], P('spec', ('groups', 'space'), None, 'vel'), parts along dimension 1
There are 2 independent parts, one for each index of `groups`. A program takes and returns all parts, laid end to end along the dimension named above; an argument that names none is the same for every part. Nothing has to cross between parts.
Inputs may be any that keep to these rules, and one draw needn't show every extreme that they name: `vel_order`: each number from 0 to 32767 appears once.
All inputs are finite; a program needn't handle non-finite values. No bound on the sum of `wall_mask` or of `inflow_mask` on one device may be relied on, other than what follows from the above.
Results may differ from a plain program's by a relative error of at most 0.0001.
Values sent between devices are 32-bit elements; how exact they have to be, the bound alone decides.
No kernel may reach another device: no remote copies, remote signals or barrier semaphores. Data moves between devices by JAX's collectives and lax.ppermute only.
A program may use at most 192 MiB of HBM per device.

v0:
```python
import jax
import jax.numpy as jnp
from jax import lax
from jax.sharding import PartitionSpec as P

NV = 32
NVEL = 32768


TIME_STEP = 0.1
RAREFACTION = 0.5
PORT_DENSITY = 1.0
HALF_RANGE = 4.5
PRECISE = lax.Precision.HIGHEST


def padded(cells, sides, width):
    for axis, dim in sides:
        count = lax.axis_size(axis)
        head = lax.slice_in_dim(cells, 0, width, axis=dim)
        tail = lax.slice_in_dim(cells, cells.shape[dim] - width, cells.shape[dim], axis=dim)
        cells = jnp.concatenate(
            [
                lax.ppermute(tail, axis, [(i, (i + 1) % count) for i in range(count)]),
                cells,
                lax.ppermute(head, axis, [((i + 1) % count, i) for i in range(count)]),
            ],
            axis=dim,
        )
    return cells


def lattice(lattice_ids, molecule_weight):
    spacing = 2.0 * HALF_RANGE / (NV - 1) / jnp.sqrt(molecule_weight)
    centre = (NV - 1) / 2.0
    index_a = (lattice_ids // (NV * NV)).astype(jnp.float32)
    index_b = (lattice_ids // NV % NV).astype(jnp.float32)
    index_e = (lattice_ids % NV).astype(jnp.float32)
    return (
        (index_a - centre) * spacing,
        (index_b - centre) * spacing,
        (index_e - centre) * spacing,
        spacing,
    )


def features(speed_x, speed_y, speed_z, molecule_weight):
    square = speed_x * speed_x + speed_y * speed_y + speed_z * speed_z
    unity = jnp.ones_like(speed_x)
    moment_rows = jnp.stack(
        [
            unity,
            molecule_weight * unity,
            molecule_weight * speed_x,
            molecule_weight * speed_y,
            molecule_weight * speed_z,
            0.5 * molecule_weight * square,
        ]
    )
    shape_rows = jnp.stack([unity, speed_x, speed_y, speed_z, square])
    return (moment_rows, shape_rows, square)


def wall_law(square, spacing, molecule_weight):
    return jnp.exp(
        jnp.log(NVEL * spacing**3)
        + 1.5 * jnp.log(molecule_weight / (2.0 * jnp.pi))
        - 0.5 * molecule_weight * square
    )


def wall_scale(molecule_weight):
    all_points = jnp.arange(NVEL, dtype=jnp.int32)
    speed_x, speed_y, speed_z, spacing = lattice(all_points, molecule_weight)
    square = speed_x * speed_x + speed_y * speed_y + speed_z * speed_z
    return jnp.sum(jnp.maximum(speed_y, 0.0) * wall_law(square, spacing, molecule_weight)) / NVEL


def mixture(first_moments, second_moments):
    blended_gas_sums_all = first_moments + second_moments
    count_per_volume = blended_gas_sums_all[0]
    component_weight_per_volume = blended_gas_sums_all[1]
    mean_drift_first = blended_gas_sums_all[2] / component_weight_per_volume
    mean_drift_second = blended_gas_sums_all[3] / component_weight_per_volume
    mean_drift_third = blended_gas_sums_all[4] / component_weight_per_volume
    motion_work_content = (
        mean_drift_first * mean_drift_first
        + mean_drift_second * mean_drift_second
        + mean_drift_third * mean_drift_third
    )
    cellwise_thermal_level = (
        2.0
        / 3.0
        * (blended_gas_sums_all[5] - 0.5 * component_weight_per_volume * motion_work_content)
        / count_per_volume
    )
    return (
        mean_drift_first,
        mean_drift_second,
        mean_drift_third,
        cellwise_thermal_level,
        count_per_volume / RAREFACTION,
    )


def coefficients(own_moments, blended_gas_mean, molecule_weight, spacing):
    (
        mean_drift_first,
        mean_drift_second,
        mean_drift_third,
        cellwise_thermal_level,
        collision_pace,
    ) = blended_gas_mean
    reciprocal_crowding = molecule_weight / cellwise_thermal_level
    motion_work_content = (
        mean_drift_first * mean_drift_first
        + mean_drift_second * mean_drift_second
        + mean_drift_third * mean_drift_third
    )
    leading = (
        jnp.log(own_moments[0])
        + jnp.log(NVEL * spacing**3)
        + 1.5 * jnp.log(reciprocal_crowding / (2.0 * jnp.pi))
        - 0.5 * reciprocal_crowding * motion_work_content
    )
    return jnp.stack(
        [
            leading,
            reciprocal_crowding * mean_drift_first,
            reciprocal_crowding * mean_drift_second,
            reciprocal_crowding * mean_drift_third,
            -0.5 * reciprocal_crowding,
        ]
    )


def collide(dist_rows, coeffs, collision_pace, shape_rows):
    exponent = lax.dot_general(
        coeffs,
        shape_rows,
        (((0,), (0,)), ((), ())),
        precision=PRECISE,
        preferred_element_type=jnp.float32,
    )
    return dist_rows + TIME_STEP * collision_pace[:, None] * (jnp.exp(exponent) - dist_rows)


def stream(collided, left_cells, right_cells, ghost_low, ghost_high, speed_x, speed_y):
    below_cells = jnp.concatenate([ghost_low[:, None, :], collided[:, :-1, :]], axis=1)
    above_cells = jnp.concatenate([collided[:, 1:, :], ghost_high[:, None, :]], axis=1)
    plus_x = jnp.maximum(speed_x, 0.0)
    minus_x = jnp.minimum(speed_x, 0.0)
    plus_y = jnp.maximum(speed_y, 0.0)
    minus_y = jnp.minimum(speed_y, 0.0)
    change = (
        plus_x * (collided - left_cells)
        + minus_x * (right_cells - collided)
        + plus_y * (collided - below_cells)
        + minus_y * (above_cells - collided)
    )
    return collided - TIME_STEP * change


def per_device(distribution, vel_order, species_mass, wall_mask, inflow_mask):
    local_dist = distribution[0]
    slab_rows, cross_rows, vel_count = local_dist.shape
    molecule_weight = species_mass.astype(jnp.float32)[0]
    speed_x, speed_y, speed_z, spacing = lattice(vel_order, molecule_weight)
    moment_rows, shape_rows, square = features(speed_x, speed_y, speed_z, molecule_weight)
    cell_count = slab_rows * cross_rows
    flat_dist = local_dist.reshape(cell_count, vel_count)
    raw_padded = padded(local_dist, (("space", 0),), 1)
    partial_value = (
        lax.dot_general(
            moment_rows,
            flat_dist,
            (((1,), (1,)), ((), ())),
            precision=PRECISE,
            preferred_element_type=jnp.float32,
        )
        / NVEL
    )
    low_flux = jnp.dot(local_dist[:, 0, :], jnp.maximum(-speed_y, 0.0), precision=PRECISE) / NVEL
    high_flux = (
        jnp.dot(local_dist[:, cross_rows - 1, :], jnp.maximum(speed_y, 0.0), precision=PRECISE)
        / NVEL
    )
    wall_part = jnp.stack([low_flux, high_flux], axis=1)
    own_moments, incident = lax.psum((partial_value, wall_part), "vel")
    gathered = lax.all_gather(own_moments[None], "spec", axis=0, tiled=True)
    first_moments = gathered[0]
    second_moments = gathered[1]
    blended_gas_mean = mixture(first_moments, second_moments)
    coeffs = coefficients(own_moments, blended_gas_mean, molecule_weight, spacing)
    collision_pace = blended_gas_mean[4]
    collided = collide(flat_dist, coeffs, collision_pace, shape_rows).reshape(
        slab_rows, cross_rows, vel_count
    )
    stacked = jnp.concatenate([coeffs, collision_pace[None]], axis=0).reshape(
        6, slab_rows, cross_rows
    )
    edge_values = padded(stacked, (("space", 1),), 1)
    low_edge = collide(raw_padded[0], edge_values[:5, 0], edge_values[5, 0], shape_rows)
    high_edge = collide(raw_padded[-1], edge_values[:5, -1], edge_values[5, -1], shape_rows)
    left_cells = jnp.concatenate([low_edge[None], collided[:-1]], axis=0)
    right_cells = jnp.concatenate([collided[1:], high_edge[None]], axis=0)
    emitted = wall_law(square, spacing, molecule_weight)
    wall_weight = wall_mask.astype(jnp.float32)
    factor = (
        wall_weight * incident / wall_scale(molecule_weight)
        + inflow_mask.astype(jnp.float32) * PORT_DENSITY
    )
    ghost_low = factor[:, 0:1] * emitted[None, :]
    ghost_high = factor[:, 1:2] * emitted[None, :]
    updated = stream(collided, left_cells, right_cells, ghost_low, ghost_high, speed_x, speed_y)
    return updated[None]


def solution(mesh):
    in_specs = (
        P("spec", ("groups", "space"), None, "vel"),
        P("vel"),
        P("spec"),
        P(("groups", "space"), None),
        P(("groups", "space"), None),
    )
    out_specs = P("spec", ("groups", "space"), None, "vel")
    return jax.shard_map(
        per_device, mesh=mesh, in_specs=in_specs, out_specs=out_specs, check_vma=False
    )
```

profile of v0, /device:TPU:0, one launch (start us, length us, event | category | flops | bytes accessed | tf_op | source)
XLA Modules:
  0.0 185.4 jit_solution(17578785017041382921)
XLA Ops:
  0.0 0.0 copy-start.1
  0.0 0.0 copy-start.2
  0.8 0.8 broadcast_minimum_fusion
  1.6 0.8 subtract_exponential_fusion
  2.5 2.6 %fusion.92 = (f32[8,1,8192]{2,1,0:T(1,128)S(1)}, f32[8,1,8192]{2,1,0:T(1,128)S(1)}) fusion(f32[8,64,8192]{2,1,0:T(8,128)} %bitcast.139), kind=kLoop, calls=%fused_computation.161 | loop fusion | bytes 1048576 | tf_op jit(solution)/shard_map/slice | solution.py:183
  5.1 0.3 stack.55
  5.4 16.6 %convolution_multiply_fusion = f32[6,512]{1,0:T(8,128)S(1)} fusion(f32[6,8192]{1,0:T(8,128)S(1)} %stack.55, f32[512,8192]{1,0:T(8,128)} %bitcast.140), kind=kOutput, calls=%fused_computation.26 | convolution fusion | flops 301992960 | bytes 16986112 | tf_op jit(solution)/shard_map/dot_general | solution.py:174
  22.0 0.7 fusion.16
  22.8 0.7 fusion.14
  23.5 20.7 %all-reduce = (f32[6,512]{1,0:T(8,128)S(1)}, f32[8,2]{0,1:T(2,128)S(1)}) all-reduce(f32[6,512]{1,0:T(8,128)S(1)} %convolution_multiply_fusion, f32[8,2]{0,1:T(2,128)S(1)} %pad_maximum_fusion), channel_id=1, replica_groups=mesh['groups'=2,'vel'=4,'space'=2,'spec'=2] {'vel'}, use_global_device_ids=true, to_apply=%region_0.1 | all-reduce | flops 3088 | bytes 24704 | tf_op jit(solution)/shard_map/psum | solution.py:189
  44.2 2.0 %all-gather.1 = f32[2,6,512]{2,1,0:T(8,128)S(1)} all-gather(f32[1,6,512]{2,1,0:T(8,128)S(1)} %bitcast.155), channel_id=2, replica_groups=mesh['groups'=2,'vel'=4,'space'=2,'spec'=2] {'spec'}, dimensions={0}, use_global_device_ids=true | all-gather | bytes 36864 | tf_op jit(solution)/shard_map/all_gather | solution.py:190
  46.3 0.5 broadcast.284
  46.8 0.7 fusion.86
  47.5 0.1 concatenate.76
  47.6 0.1 concatenate.78
  47.7 0.1 concatenate.77
  47.7 0.1 concatenate.75
  47.8 0.1 concatenate.74
  47.9 0.1 concatenate.73
  48.0 1.6 collective-permute-start.3
  49.6 0.5 collective-permute-start.1
  50.1 3.9 %slice_bitcast_fusion.2 = (f32[1,64,8192]{2,1,0:T(8,128)S(1)}, f32[1,64,8192]{2,1,0:T(8,128)}) fusion(f32[1,8,64,8192]{3,2,1,0:T(8,128)} %param.5), kind=kLoop, calls=%fused_computation.24 | loop fusion | bytes 8388608 | tf_op jit(solution)/shard_map/slice | solution.py:20
  54.0 1.5 collective-permute-start.2
  55.5 0.5 collective-permute-start
  56.0 0.7 fusion.48
  57.4 0.0 copy-done.1
  57.4 0.0 copy-done.2
  57.5 0.2 stack.61
  57.7 19.3 %multiply_add_fusion = f32[512,8192]{1,0:T(8,128)S(1)} fusion(f32[512,8192]{1,0:T(8,128)} %bitcast.141, f32[5,512]{1,0:T(8,128)S(1)} %stack.56, f32[5,8192]{1,0:T(8,128)S(1)} %stack.61, f32[512]{0:T(512)S(1)} %bitcast.154), kind=kOutput, calls=%fused_computation.15 | convolution fusion | flops 264241152 | bytes 33730560 | tf_op jit(solution)/shard_map/dot_general | solution.py:138
  77.0 0.0 copy-start
  77.1 10.4 %fusion.91 = (f32[448,8192]{1,0:T(8,128)}, f32[448,8192]{1,0:T(8,128)}) fusion(f32[512,8192]{1,0:T(8,128)S(1)} %multiply_add_fusion), kind=kLoop, calls=%fused_computation.160 | loop fusion | bytes 58720256 | tf_op jit(solution)/shard_map/slice | solution.py:206
  87.4 4.6 %copy-done = f32[512,8192]{1,0:T(8,128)} copy-done((f32[512,8192]{1,0:T(8,128)}, f32[512,8192]{1,0:T(8,128)S(1)}, u32[]{:S(2)}) %copy-start) | copy-done | bytes 16777240
  92.0 11.7 %slice_bitcast_fusion = (f32[1,8,63,8192]{3,2,1,0:T(8,128)}, f32[1,8,63,8192]{3,2,1,0:T(8,128)}) fusion(f32[8,64,8192]{2,1,0:T(8,128)S(1)} %bitcast.137), kind=kLoop, calls=%fused_computation | loop fusion | bytes 66060288 | tf_op jit(solution)/shard_map/concatenate | solution.py:150
  103.7 0.4 multiply_bitcast_fusion
  104.2 0.0 collective-permute-done.3
  104.2 0.0 collective-permute-done.1
  104.2 0.0 collective-permute-done.2
  104.2 3.8 %fusion.11 = f32[1,1,64,8192]{3,2,1,0:T(8,128)S(1)} fusion(f32[1,64,8192]{2,1,0:T(8,128)} %collective-permute-done.2, f32[64]{0:T(128)S(1)} %fusion.78, f32[5,8192]{1,0:T(8,128)S(1)} %stack.61, f32[5,1,64]{2,1,0:T(1,128)S(1)} %slice.145), kind=kOutput, calls=%fused_computation.21 | convolution fusion | flops 33030144 | bytes 4359680 | tf_op jit(solution)/shard_map/dot_general | solution.py:138
  108.0 38.2 %collective-permute-done = f32[1,64,8192]{2,1,0:T(8,128)} collective-permute-done((f32[1,64,8192]{2,1,0:T(8,128)}, f32[1,64,8192]{2,1,0:T(8,128)}, u32[]{:S(2)}, u32[]{:S(2)}) %collective-permute-start) | collective-permute-done | bytes 2097184 | tf_op jit(solution)/shard_map/ppermute | solution.py:24
  146.2 5.1 %fusion.12 = f32[1,1,64,8192]{3,2,1,0:T(8,128)} fusion(f32[1,64,8192]{2,1,0:T(8,128)} %collective-permute-done, f32[64]{0:T(128)S(1)} %fusion.79, f32[5,8192]{1,0:T(8,128)S(1)} %stack.61, f32[5,1,64]{2,1,0:T(1,128)S(1)} %slice.140), kind=kOutput, calls=%fused_computation.23 | convolution fusion | flops 33030144 | bytes 4359680 | tf_op jit(solution)/shard_map/dot_general | solution.py:138
  151.3 34.1 %fusion.5 = f32[1,8,64,8192]{3,2,1,0:T(8,128)} fusion(f32[1,8,64,8192]{3,2,1,0:T(8,128)} %bitcast.138, f32[1,7,64,8192]{3,2,1,0:T(8,128)} %bitcast.143, f32[1,1,64,8192]{3,2,1,0:T(8,128)} %fusion.12, f32[1,1,64,8192]{3,2,1,0:T(8,128)S(1)} %fusion.11, f32[1,7,64,8192]{3,2,1,0:T(8,128)} %bitcast.142, f32[1,8,63,8192]{3,2,1,0:T(8,128)} %get-tuple-element.30, ...), kind=kLoop, calls=%fused_computation.8 | loop fusion | flops 71303168 | bytes 100794368 | tf_op jit(solution)/shard_map/sub | solution.py:161
  (21 shorter events, 0.2 us)
Async XLA Ops:
  0.0 57.4 %copy-start.1 = (s32[8,2]{0,1:T(2,128)S(1)}, s32[8,2]{0,1:T(2,128)}, u32[]{:S(2)}) copy-start(s32[8,2]{0,1:T(2,128)} %param.9) | copy-start | bytes 196
  0.0 57.4 %copy-start.2 = (s32[8,2]{0,1:T(2,128)S(1)}, s32[8,2]{0,1:T(2,128)}, u32[]{:S(2)}) copy-start(s32[8,2]{0,1:T(2,128)} %param.8) | copy-start | bytes 196
  48.0 56.2 %collective-permute-start.3 = (f32[6,1,64]{2,1,0:T(1,128)S(1)}, f32[6,1,64]{2,1,0:T(1,128)S(1)}, u32[]{:S(2)}, u32[]{:S(2)}) collective-permute-start(f32[6,1,64]{2,1,0:T(1,128)S(1)} %get-tuple-element.46), channel_id=1, source_target_pairs={{2,0},{0,2},{3,1},{1,3},{6,4},{4,6},{7,5},{5,7},{10,8},{8,10},{11,... | collective-permute-start | bytes 4616 | tf_op jit(solution)/shard_map/ppermute | solution.py:26
  49.6 54.6 %collective-permute-start.1 = (f32[6,1,64]{2,1,0:T(1,128)S(1)}, f32[6,1,64]{2,1,0:T(1,128)S(1)}, u32[]{:S(2)}, u32[]{:S(2)}) collective-permute-start(f32[6,1,64]{2,1,0:T(1,128)S(1)} %get-tuple-element.47), channel_id=1, source_target_pairs={{0,2},{2,0},{1,3},{3,1},{4,6},{6,4},{5,7},{7,5},{8,10},{10,8},{9,1... | collective-permute-start | bytes 4616 | tf_op jit(solution)/shard_map/ppermute | solution.py:24
  54.0 50.2 %collective-permute-start.2 = (f32[1,64,8192]{2,1,0:T(8,128)S(1)}, f32[1,64,8192]{2,1,0:T(8,128)}, u32[]{:S(2)}, u32[]{:S(2)}) collective-permute-start(f32[1,64,8192]{2,1,0:T(8,128)S(1)} %get-tuple-element.33), channel_id=1, source_target_pairs={{2,0},{0,2},{3,1},{1,3},{6,4},{4,6},{7,5},{5,7},{10,8},{8,10},{11,... | collective-permute-start | bytes 6291464 | tf_op jit(solution)/shard_map/ppermute | solution.py:26
  55.5 90.7 %collective-permute-start = (f32[1,64,8192]{2,1,0:T(8,128)}, f32[1,64,8192]{2,1,0:T(8,128)}, u32[]{:S(2)}, u32[]{:S(2)}) collective-permute-start(f32[1,64,8192]{2,1,0:T(8,128)} %get-tuple-element.34), channel_id=1, source_target_pairs={{0,2},{2,0},{1,3},{3,1},{4,6},{6,4},{5,7},{7,5},{8,10},{10,8},{9,1... | collective-permute-start | bytes 6291464 | tf_op jit(solution)/shard_map/ppermute | solution.py:24
  77.0 15.0 %copy-start = (f32[512,8192]{1,0:T(8,128)}, f32[512,8192]{1,0:T(8,128)S(1)}, u32[]{:S(2)}) copy-start(f32[512,8192]{1,0:T(8,128)S(1)} %multiply_add_fusion) | copy-start | bytes 50331652
where the time goes:
time: 186 us; the launch traced here: 185 us
  matrix products  46.2 us (25%)
  waiting for transfers between devices  38.2 us (21%)
  other arithmetic  37.7 us (20%)
  local copies, waits for them, and re-layouts  34.8 us (19%)
  blocking collectives  22.7 us (12%)
  starting transfers between devices  4.12 us (2%)
    ppermute x2, waiting for transfers between devices, padded(): lax.ppermute(tail, axis, [(i, (i + 1) % count) for i in range(count)])  38.2 us
    sub x1, other arithmetic, stream(): return collided - TIME_STEP * change  34.1 us
    dot_general x3, matrix products, collide(): lax.dot_general(coeffs, shape_rows, (((0,), (0,)), ((), ())), precision=P...  28.2 us
    psum x1, blocking collectives, per_device(): own_moments, incident = lax.psum((partial_value, wall_part), 'vel')  20.7 us
    dot_general x1, matrix products, per_device(): lax.dot_general(moment_rows, flat_dist, (((1,), (1,)), ((), ())), precisi...  16.6 us
    concatenate x1, local copies, waits for them, and re-layouts, stream(): jnp.concatenate([collided[:, 1:, :], ghost_high[:, None, :]], axis=1)  11.7 us
    slice x1, local copies, waits for them, and re-layouts, per_device(): right_cells = jnp.concatenate([collided[1:], high_edge[None]], axis=0)  10.4 us
    unnamed x11, local copies, waits for them, and re-layouts  4.62 us
  transfers between devices with their start and end apart: 4, of which 1 were waited for; matrix products, arithmetic and copies ran while one was open for 27% of the time, Pallas kernels for 0%

commit v1 on v0

v1 whole, which is shorter than its diff:
```python
import math

import jax
import jax.numpy as jnp
import numpy as np
from jax import lax
from jax.experimental import pallas as pl
from jax.experimental.pallas import tpu as pltpu
from jax.sharding import PartitionSpec as P


NV = 32
NVEL = 32768

TIME_STEP = 0.1
RAREFACTION = 0.5
PORT_DENSITY = 1.0
HALF_RANGE = 4.5

LANES = 128
VMEM_LIMIT = 50 * 2**20
LOG2E = math.log2(math.e)
STEP = 2.0 * HALF_RANGE / (NV - 1)
ODD = 2.0 * np.arange(NV) - (NV - 1)
LAW_FRONT = NVEL * STEP**3 / (2.0 * math.pi) ** 1.5
LAW_RATE = STEP * STEP / 8.0
LAW_AXIS = np.exp(-LAW_RATE * ODD**2)
LAW_HALF = float(
    LAW_FRONT * 0.5 * STEP * np.sum(np.maximum(ODD, 0.0) * LAW_AXIS) * np.sum(LAW_AXIS) ** 2 / NVEL
)


def lattice_rows(ids):
    x = (2 * (ids // (NV * NV)) - (NV - 1)).astype(jnp.float32)
    y = (2 * (ids // NV % NV) - (NV - 1)).astype(jnp.float32)
    z = (2 * (ids % NV) - (NV - 1)).astype(jnp.float32)
    return x, y, z


def moments_kernel(mass_ref, ids_ref, dist_ref, rows_ref, part_ref, feat):
    vel = ids_ref.shape[1]
    cross = dist_ref.shape[1]
    tiles = vel // LANES
    groups = cross // 8
    mass = jnp.full((8, LANES), mass_ref[0], jnp.int32).astype(jnp.float32)
    half = 0.5 * STEP / jnp.sqrt(mass)

    @pl.when(pl.program_id(0) == 0)
    def _():
        def fill(t, carry):
            at = pl.ds(pl.multiple_of(t * LANES, LANES), LANES)
            ids = jnp.broadcast_to(ids_ref[:, at], (8, LANES))
            x, y, z = lattice_rows(ids)
            square = x * x + y * y + z * z
            high = square.astype(jnp.bfloat16).astype(jnp.float32)
            feat[0, :, at] = x
            feat[1, :, at] = y
            feat[2, :, at] = z
            feat[3, :, at] = square
            row = lax.broadcasted_iota(jnp.int32, (8, LANES), 0)
            out = jnp.where(row == 0, 1.0, x)
            out = jnp.where(row == 2, y, out)
            out = jnp.where(row == 3, z, out)
            out = jnp.where(row == 4, high, out)
            out = jnp.where(row == 5, square - high, out)
            out = jnp.where(row == 6, TIME_STEP * half * jnp.abs(x), out)
            out = jnp.where(row == 7, TIME_STEP * half * jnp.abs(y), out)
            rows_ref[:, at] = out
            return carry

        lax.fori_loop(0, tiles, fill, 0)

    def step(t, carry):
        sums, low, high = carry
        at = pl.ds(pl.multiple_of(t * LANES, LANES), LANES)
        x = feat[0, :, at]
        y = feat[1, :, at]
        z = feat[2, :, at]
        square = feat[3, :, at]
        new = []
        for g in range(groups):
            f = dist_ref[0, 8 * g : 8 * g + 8, at]
            n, mx, my, mz, e = sums[g]
            fy = f * y
            new.append((n + f, mx + f * x, my + fy, mz + f * z, e + f * square))
            if g == 0:
                low = low + jnp.maximum(-fy, 0.0)
            if g == groups - 1:
                high = high + jnp.maximum(fy, 0.0)
        return tuple(new), low, high

    zero = jnp.zeros((8, LANES), jnp.float32)
    sums, low, high = lax.fori_loop(
        0, tiles, step, (tuple((zero,) * 5 for _ in range(groups)), zero, zero)
    )
    scales = (
        jnp.full((8, LANES), 1.0 / NVEL, jnp.float32),
        mass * half / NVEL,
        mass * half / NVEL,
        mass * half / NVEL,
        0.5 * mass * half * half / NVEL,
        half / NVEL,
        mass / NVEL,
    )
    columns = [[sums[g][j] for g in range(groups)] for j in range(5)]
    columns.append([low] + [zero] * (groups - 2) + [high])
    columns.append(columns[0])
    row = lax.broadcasted_iota(jnp.int32, (8, LANES), 0)
    total = jnp.zeros((8, cross), jnp.float32)
    for j in range(7):
        picked = jnp.where(row == j, 1.0, 0.0)
        summed = lax.dot_general(
            picked,
            jnp.concatenate(columns[j], axis=0),
            (((1,), (1,)), ((), ())),
            precision=lax.Precision.HIGHEST,
            preferred_element_type=jnp.float32,
        )
        total = total + summed * scales[j][:, :cross]
    part_ref[0] = total


def moments(mass, ids, dist):
    rows, cross, vel = dist.shape
    return pl.pallas_call(
        moments_kernel,
        name="moments",
        grid=(rows,),
        in_specs=[
            pl.BlockSpec(memory_space=pltpu.SMEM),
            pl.BlockSpec((1, vel), lambda i: (0, 0)),
            pl.BlockSpec((1, cross, vel), lambda i: (i, 0, 0)),
        ],
        out_specs=[
            pl.BlockSpec((8, vel), lambda i: (0, 0)),
            pl.BlockSpec((1, 8, cross), lambda i: (i, 0, 0)),
        ],
        out_shape=[
            jax.ShapeDtypeStruct((8, vel), jnp.float32),
            jax.ShapeDtypeStruct((rows, 8, cross), jnp.float32),
        ],
        scratch_shapes=[pltpu.VMEM((4, 8, vel), jnp.float32)],
        compiler_params=pltpu.CompilerParams(
            dimension_semantics=("arbitrary",), vmem_limit_bytes=VMEM_LIMIT
        ),
    )(mass, ids, dist)


def coefficients_kernel(mass_ref, own_ref, other_ref, wall_ref, port_ref, coef_ref, fac_ref):
    rows, _, cross = own_ref.shape
    own = own_ref[...]
    total = own + other_ref[...]
    mass = jnp.full((rows, cross), mass_ref[0], jnp.int32).astype(jnp.float32)
    half = 0.5 * STEP / jnp.sqrt(mass)
    n = total[:, 0]
    r = total[:, 6]
    ux = total[:, 1] / r
    uy = total[:, 2] / r
    uz = total[:, 3] / r
    speed = ux * ux + uy * uy + uz * uz
    temperature = (2.0 / 3.0) * (total[:, 4] - 0.5 * r * speed) / n
    weight = TIME_STEP * (n / RAREFACTION)
    beta = mass / temperature
    leading = (
        jnp.log(own[:, 0])
        + math.log(LAW_FRONT)
        - 1.5 * jnp.log(temperature)
        - 0.5 * beta * speed
        + jnp.log(weight)
    )
    scale = LOG2E * beta * half
    square = -0.5 * scale * half
    coef_ref[:, 0] = LOG2E * leading
    coef_ref[:, 1] = scale * ux
    coef_ref[:, 2] = scale * uy
    coef_ref[:, 3] = scale * uz
    coef_ref[:, 4] = square
    coef_ref[:, 5] = square
    coef_ref[:, 6] = 1.0 - weight
    coef_ref[:, 7] = jnp.zeros_like(weight)
    wall = wall_ref[...].astype(jnp.float32)
    port = port_ref[...].astype(jnp.float32)
    incident = own[:, 5]
    share = jnp.sqrt(mass[:, :1]) / LAW_HALF
    for side, cell in ((0, 0), (1, cross - 1)):
        factor = (
            wall[:, side : side + 1] * incident[:, cell : cell + 1] * share
            + port[:, side : side + 1] * PORT_DENSITY
        )
        fac_ref[:, side] = jnp.broadcast_to(factor, (rows, LANES))


def coefficients(mass, own, other, wall_mask, inflow_mask):
    rows, _, cross = own.shape
    return pl.pallas_call(
        coefficients_kernel,
        name="coefficients",
        in_specs=[pl.BlockSpec(memory_space=pltpu.SMEM)]
        + [pl.BlockSpec(memory_space=pltpu.VMEM)] * 4,
        out_specs=[pl.BlockSpec(memory_space=pltpu.VMEM)] * 2,
        out_shape=[
            jax.ShapeDtypeStruct((rows, 8, cross), jnp.float32),
            jax.ShapeDtypeStruct((rows, 2, LANES), jnp.float32),
        ],
        compiler_params=pltpu.CompilerParams(vmem_limit_bytes=VMEM_LIMIT),
    )(mass, own, other, wall_mask, inflow_mask)


def split_columns(coef):
    row = lax.broadcasted_iota(jnp.int32, coef.shape, 0)
    rest = jnp.where(row < 6, coef, 0.0)
    pieces = []
    for _ in range(3):
        piece = rest.astype(jnp.bfloat16).astype(jnp.float32)
        pieces.append(piece)
        rest = rest - piece
    pieces.append(jnp.zeros_like(coef))
    return jnp.concatenate(pieces, axis=0).T.astype(jnp.bfloat16)


def split_rows(rows):
    return jnp.concatenate([rows, rows, rows, jnp.zeros_like(rows)], axis=0).astype(jnp.bfloat16)


def keep_column(coef, width):
    return jnp.broadcast_to(coef.T[:, 6:7], (coef.shape[1], width))


def slab_kernel(coef_ref, fac_ref, rows_ref, dist_ref, out_ref, table, keep):
    slab, cross, width = dist_ref.shape

    @pl.when(pl.program_id(0) == 0)
    def _():
        for x in range(slab):
            table[x] = split_columns(coef_ref[x])
            keep[x] = keep_column(coef_ref[x], LANES)

    def step(t, carry):
        at = pl.ds(pl.multiple_of(t * LANES, LANES), LANES)
        rows = rows_ref[:, at]
        shape = split_rows(rows)
        plus_x = rows[1:2] > 0.0
        plus_y = rows[2:3] > 0.0
        ax = rows[6:7]
        ay = rows[7:8]
        stay = 1.0 - ax - ay
        emitted = LAW_FRONT * jnp.exp2(-(LAW_RATE * LOG2E) * (rows[4:5] + rows[5:6]))
        row = lax.broadcasted_iota(jnp.int32, (cross, LANES), 0)

        def collided(x):
            exponent = jnp.dot(table[x], shape, preferred_element_type=jnp.float32)
            return dist_ref[x, :, at] * keep[x] + jnp.exp2(exponent)

        left = jnp.zeros((cross, LANES), jnp.float32)
        here = collided(0)
        for x in range(slab):
            right = collided(x + 1) if x + 1 < slab else jnp.zeros((cross, LANES), jnp.float32)
            below = jnp.where(row == 0, fac_ref[x, 0:1] * emitted, pltpu.roll(here, 1, axis=0))
            above = jnp.where(
                row == cross - 1, fac_ref[x, 1:2] * emitted, pltpu.roll(here, cross - 1, axis=0)
            )
            out_ref[x, :, at] = (
                stay * here
                + ax * jnp.where(plus_x, left, right)
                + ay * jnp.where(plus_y, below, above)
            )
            left, here = here, right
        return carry

    lax.fori_loop(0, width // LANES, step, 0)


def slab_update(coef, fac, rows, dist, width):
    slab, cross, vel = dist.shape
    return pl.pallas_call(
        slab_kernel,
        name="slab_update",
        grid=(vel // width,),
        in_specs=[
            pl.BlockSpec((slab, 8, cross), lambda k: (0, 0, 0)),
            pl.BlockSpec((slab, 2, LANES), lambda k: (0, 0, 0)),
            pl.BlockSpec((8, width), lambda k: (0, k)),
            pl.BlockSpec((slab, cross, width), lambda k: (0, 0, k)),
        ],
        out_specs=pl.BlockSpec((slab, cross, width), lambda k: (0, 0, k)),
        out_shape=jax.ShapeDtypeStruct((slab, cross, vel), jnp.float32),
        scratch_shapes=[
            pltpu.VMEM((slab, cross, 32), jnp.bfloat16),
            pltpu.VMEM((slab, cross, LANES), jnp.float32),
        ],
        compiler_params=pltpu.CompilerParams(
            dimension_semantics=("arbitrary",), vmem_limit_bytes=VMEM_LIMIT
        ),
    )(coef, fac, rows, dist)


def edge_kernel(left_ref, right_ref, rows_ref, halo_ref, in_ref, out_ref, gain):
    _, width = halo_ref.shape
    side = pl.program_id(1)

    @pl.when(side == 0)
    def _():
        table = jnp.concatenate(
            [split_columns(left_ref[...]), split_columns(right_ref[...])], axis=1
        )
        keep_left = keep_column(left_ref[...], LANES)
        keep_right = keep_column(right_ref[...], LANES)

        def step(t, carry):
            at = pl.ds(pl.multiple_of(t * LANES, LANES), LANES)
            rows = rows_ref[:, at]
            plus = rows[1:2] > 0.0
            shape = jnp.concatenate(
                [
                    split_rows(jnp.where(plus, rows, 0.0)),
                    split_rows(jnp.where(plus, 0.0, rows)),
                ],
                axis=0,
            )
            exponent = jnp.dot(table, shape, preferred_element_type=jnp.float32)
            value = rows[6:7] * (
                halo_ref[:, at] * jnp.where(plus, keep_left, keep_right) + jnp.exp2(exponent)
            )
            gain[:, at] = value
            out_ref[0, :, at] = in_ref[0, :, at] + jnp.where(plus, value, 0.0)
            return carry

        lax.fori_loop(0, width // LANES, step, 0)

    @pl.when(side == 1)
    def _():
        def step(t, carry):
            at = pl.ds(pl.multiple_of(t * LANES, LANES), LANES)
            plus = rows_ref[1:2, at] > 0.0
            out_ref[0, :, at] = in_ref[0, :, at] + jnp.where(plus, 0.0, gain[:, at])
            return carry

        lax.fori_loop(0, width // LANES, step, 0)


def edge_update(left, right, rows, halo, updated, start, width):
    slab, cross, _ = updated.shape
    first = start // width
    return pl.pallas_call(
        edge_kernel,
        name="edge_update",
        grid=(halo.shape[1] // width, 2),
        in_specs=[
            pl.BlockSpec((8, cross), lambda k, s: (0, 0)),
            pl.BlockSpec((8, cross), lambda k, s: (0, 0)),
            pl.BlockSpec((8, width), lambda k, s: (0, first + k)),
            pl.BlockSpec((cross, width), lambda k, s: (0, k)),
            pl.BlockSpec((1, cross, width), lambda k, s: (s * (slab - 1), 0, first + k)),
        ],
        out_specs=pl.BlockSpec((1, cross, width), lambda k, s: (s * (slab - 1), 0, first + k)),
        out_shape=jax.ShapeDtypeStruct(updated.shape, jnp.float32),
        scratch_shapes=[pltpu.VMEM((cross, width), jnp.float32)],
        input_output_aliases={4: 0},
        compiler_params=pltpu.CompilerParams(
            dimension_semantics=("arbitrary", "arbitrary"), vmem_limit_bytes=VMEM_LIMIT
        ),
    )(left, right, rows, halo, updated)


def select_kernel(ids_ref, tail_ref, head_ref, out_ref):
    plus = ids_ref[...] >= NV * NV * NV // 2
    out_ref[...] = jnp.where(plus, tail_ref[0], head_ref[0])


def select_edges(ids, dist, after, start, end, width):
    slab, cross, _ = dist.shape
    first = start // width
    gates = [] if after is None else [after]

    def kernel(*refs):
        select_kernel(*refs[len(gates) :])

    return pl.pallas_call(
        kernel,
        name="select_edges",
        grid=((end - start) // width,),
        in_specs=[pl.BlockSpec(memory_space=pl.ANY)] * len(gates)
        + [
            pl.BlockSpec((1, width), lambda k: (0, first + k)),
            pl.BlockSpec((1, cross, width), lambda k: (slab - 1, 0, first + k)),
            pl.BlockSpec((1, cross, width), lambda k: (0, 0, first + k)),
        ],
        out_specs=pl.BlockSpec((cross, width), lambda k: (0, k)),
        out_shape=jax.ShapeDtypeStruct((cross, end - start), jnp.float32),
        compiler_params=pltpu.CompilerParams(
            dimension_semantics=("arbitrary",), vmem_limit_bytes=VMEM_LIMIT
        ),
    )(*gates, ids, dist, dist)


def both_ways(tail, head, axis):
    count = lax.axis_size(axis)
    if count == 1:
        return tail, head
    return (
        lax.ppermute(tail, axis, [(i, (i + 1) % count) for i in range(count)]),
        lax.ppermute(head, axis, [((i + 1) % count, i) for i in range(count)]),
    )


def edge_cells(ids, dist, after, start, end, width, axis):
    count = lax.axis_size(axis)
    if count > 2:
        tail, head = dist[-1, :, start:end], dist[0, :, start:end]
        if after is not None:
            tail, head = lax.optimization_barrier((tail, head, after))[:2]
        from_left, from_right = both_ways(tail, head, axis)
        return jnp.where(ids[:, start:end] >= NV * NV * NV // 2, from_left, from_right)
    chosen = select_edges(ids, dist, after, start, end, width)
    if count == 2:
        chosen = lax.ppermute(chosen, axis, [(0, 1), (1, 0)])
    return chosen


def edge_coefficients(coef, axis):
    count = lax.axis_size(axis)
    if count == 2:
        pair = lax.ppermute(jnp.stack([coef[-1], coef[0]]), axis, [(0, 1), (1, 0)])
        return pair[0], pair[1]
    return both_ways(coef[-1], coef[0], axis)


def summed(part, axis):
    count = lax.axis_size(axis)
    if count & (count - 1):
        return lax.psum(part, axis)
    step = 1
    while step < count:
        part = part + lax.ppermute(part, axis, [(i, i ^ step) for i in range(count)])
        step *= 2
    return part


def chunk_ends(tiles):
    ends = sorted({max(1, tiles // 16), tiles // 2, tiles - max(1, tiles // 8), tiles})
    return [LANES * end for end in ends]


def body(distribution, vel_order, species_mass, wall_mask, inflow_mask):
    dist = distribution[0]
    _, _, vel = dist.shape
    ids = vel_order[None]
    ends = chunk_ends(vel // LANES)
    starts = [0] + ends[:-1]
    widths = [min(math.gcd(start, end - start) if start else end, 1024) for start, end in zip(starts, ends)]
    halos = []
    for start, end, width in zip(starts, ends, widths):
        if end <= vel // 2:
            halos.append(edge_cells(ids, dist, None, start, end, width, "space"))
    rows, part = moments(species_mass, ids, dist)
    own = summed(part, "vel")
    other = lax.ppermute(own, "spec", [(0, 1), (1, 0)])
    coef, fac = coefficients(species_mass, own, other, wall_mask, inflow_mask)
    left, right = edge_coefficients(coef, "space")
    for start, end, width in zip(starts, ends, widths):
        if end > vel // 2:
            halos.append(edge_cells(ids, dist, coef, start, end, width, "space"))
    updated = slab_update(coef, fac, rows, dist, min(vel, 512))
    for start, halo, width in zip(starts, halos, widths):
        updated = edge_update(left, right, rows, halo, updated, start, width)
    return updated[None]


def solution(mesh):
    in_specs = (
        P("spec", ("groups", "space"), None, "vel"),
        P("vel"),
        P("spec"),
        P(("groups", "space"), None),
        P(("groups", "space"), None),
    )
    out_specs = P("spec", ("groups", "space"), None, "vel")
    return jax.shard_map(body, mesh=mesh, in_specs=in_specs, out_specs=out_specs, check_vma=False)
```

time: 186 us -> 97.9 us (0.53)
  Pallas kernels: 0 us -> 78 us
  matrix products: 46.2 us -> 0 us
  other arithmetic: 37.7 us -> 0.02 us
  local copies, waits for them, and re-layouts: 34.8 us -> 0.94 us
  waiting for transfers between devices: 38.2 us -> 5.6 us
  blocking collectives: 22.7 us -> 0 us
  starting transfers between devices: 4.12 us -> 11.5 us
    pallas_call x0 -> x11, Pallas kernels: none -> 78 us  [the longest x4 26.3 us: edge_update(): pl.pallas_call(edge_kernel, name='edge_update', grid=(halo.shape[1] // wi...]
    dot_general x6 -> x0, matrix products: 46.2 us -> none  [the longest x3 28.2 us: collide(): lax.dot_general(coeffs, shape_rows, (((0,), (0,)), ((), ())), precision=P...]
    sub x1 -> x0, other arithmetic: 34.1 us -> none  [stream(): return collided - TIME_STEP * change]
    ppermute x4 -> x8, waiting for transfers between devices: 38.2 us -> 5.6 us  [the longest x2 4.56 us: summed(): lax.ppermute(part, axis, [(i, i ^ step) for i in range(count)])]
    psum x1 -> x0, blocking collectives: 20.7 us -> none  [per_device(): own_moments, incident = lax.psum((partial_value, wall_part), 'vel')]
    slice x7 -> x1, local copies, waits for them, and re-layouts: 16.9 us -> 0.01 us  [edge_coefficients(): pair = lax.ppermute(jnp.stack([coef[-1], coef[0]]), axis, [(0, 1), (1, 0)])]
    concatenate x8 -> x0, local copies, waits for them, and re-layouts: 12.1 us -> none  [the longest x1 11.7 us: stream(): jnp.concatenate([collided[:, 1:, :], ghost_high[:, None, :]], axis=1)]
    ppermute x4 -> x8, starting transfers between devices: 4.12 us -> 11.5 us  [the longest x4 7.08 us: edge_cells(): chosen = lax.ppermute(chosen, axis, [(0, 1), (1, 0)])]
  transfers between devices with their start and end apart: 4 -> 8, of which waited for: 1 -> 3; matrix products, arithmetic and copies ran while one was open for 27% -> 0% of each run, Pallas kernels for 0% -> 73%
where the time goes in v1:
time: 97.9 us; the launch traced here: 96.8 us
  Pallas kernels  78 us (80%)
  starting transfers between devices  11.5 us (12%)
  waiting for transfers between devices  5.6 us (6%)
    pallas_call x4, Pallas kernels, edge_update(): pl.pallas_call(edge_kernel, name='edge_update', grid=(halo.shape[1] // wi...  26.3 us
    pallas_call x1, Pallas kernels, slab_update(): pl.pallas_call(slab_kernel, name='slab_update', grid=(vel // width,), in_...  24.4 us
    pallas_call x1, Pallas kernels, moments(): pl.pallas_call(moments_kernel, name='moments', grid=(rows,), in_specs=[pl...  18.8 us
    pallas_call x4, Pallas kernels, select_edges(): pl.pallas_call(kernel, name='select_edges', grid=((end - start) // width,...  8.36 us
    ppermute x4, starting transfers between devices, edge_cells(): chosen = lax.ppermute(chosen, axis, [(0, 1), (1, 0)])  7.08 us
    ppermute x2, waiting for transfers between devices, summed(): lax.ppermute(part, axis, [(i, i ^ step) for i in range(count)])  4.56 us
    ppermute x2, starting transfers between devices, summed(): lax.ppermute(part, axis, [(i, i ^ step) for i in range(count)])  4.19 us
  transfers between devices with their start and end apart: 8, of which 3 were waited for; matrix products, arithmetic and copies ran while one was open for 0% of the time, Pallas kernels for 73%

profile of v1, /device:TPU:0, one launch (start us, length us, event | category | flops | bytes accessed | tf_op | source)
XLA Modules:
  0.0 96.8 jit_solution(10298487609546109932)
XLA Ops:
  0.0 0.0 copy-start
  0.0 0.8 copy-done
  0.8 4.1 %select_edges.6 = f32[64,3584]{1,0:T(8,128)S(1)} custom-call(s32[1,8192]{1,0:T(1,128)S(1)} %bitcast.7, f32[8,64,8192]{2,1,0:T(8,128)} %bitcast.12, f32[8,64,8192]{2,1,0:T(8,128)} %bitcast.13), custom_call_target="tpu_custom_call" | custom-call | tf_op jit(solution)/shard_map/select_edges/pallas_call | solution.py:378
  4.9 0.0 copy-start.2
  4.9 0.0 copy-start.3
  4.9 0.0 copy-start.1
  4.9 3.0 %collective-permute-start.6 = (f32[64,3584]{1,0:T(8,128)S(1)}, f32[64,3584]{1,0:T(8,128)S(1)}, u32[]{:S(2)}, u32[]{:S(2)}) collective-permute-start(f32[64,3584]{1,0:T(8,128)S(1)} %select_edges.6), channel_id=1, source_target_pairs={{0,2},{2,0},{1,3},{3,1},{4,6},{6,4},{5,7},{7,5},{8,10},{10,8},{9,1... | collective-permute-start | bytes 2752520 | tf_op jit(solution)/shard_map/ppermute | solution.py:416
  8.6 18.8 %moments.1 = (f32[8,8192]{1,0:T(8,128)S(1)}, f32[8,8,64]{2,1,0:T(8,128)S(1)}) custom-call(s32[1]{0:T(128)S(6)} %copy.16.mass_ref, s32[1,8192]{1,0:T(1,128)S(1)} %bitcast.8, f32[8,64,8192]{2,1,0:T(8,128)} %bitcast.14), custom_call_target="tpu_custom_call" | custom-call | tf_op jit(solution)/shard_map/moments/pallas_call | solution.py:125
  27.4 1.6 %collective-permute-start = (f32[8,8,64]{2,1,0:T(8,128)S(1)}, f32[8,8,64]{2,1,0:T(8,128)S(1)}, u32[]{:S(2)}, u32[]{:S(2)}) collective-permute-start(f32[8,8,64]{2,1,0:T(8,128)S(1)} %get-tuple-element.9), channel_id=1, source_target_pairs={{0,4},{4,0},{8,12},{12,8},{1,5},{5,1},{9,13},{13,9},{2,6},{6,2},{1... | collective-permute-start | bytes 49160 | tf_op jit(solution)/shard_map/ppermute | solution.py:434
  29.0 2.3 %collective-permute-done = f32[8,8,64]{2,1,0:T(8,128)S(1)} collective-permute-done((f32[8,8,64]{2,1,0:T(8,128)S(1)}, f32[8,8,64]{2,1,0:T(8,128)S(1)}, u32[]{:S(2)}, u32[]{:S(2)}) %collective-permute-start) | collective-permute-done | bytes 16416 | tf_op jit(solution)/shard_map/ppermute | solution.py:434
  31.3 2.6 %collective-permute-start.1 = (f32[8,8,64]{2,1,0:T(8,128)S(1)}, f32[8,8,64]{2,1,0:T(8,128)S(1)}, u32[]{:S(2)}, u32[]{:S(2)}) collective-permute-start(f32[8,8,64]{2,1,0:T(8,128)S(1)} %add.6), channel_id=1, source_target_pairs={{0,8},{4,12},{8,0},{12,4},{1,9},{5,13},{9,1},{13,5},{2,10},{6,14},... | collective-permute-start | bytes 49160 | tf_op jit(solution)/shard_map/ppermute | solution.py:434
  33.9 2.2 %collective-permute-done.1 = f32[8,8,64]{2,1,0:T(8,128)S(1)} collective-permute-done((f32[8,8,64]{2,1,0:T(8,128)S(1)}, f32[8,8,64]{2,1,0:T(8,128)S(1)}, u32[]{:S(2)}, u32[]{:S(2)}) %collective-permute-start.1) | collective-permute-done | bytes 16416 | tf_op jit(solution)/shard_map/ppermute | solution.py:434
  36.2 0.0 collective-permute-start.2
  36.2 0.0 copy-done.2
  36.2 0.1 copy.10.wall_ref
  36.3 0.0 copy-done.3
  36.3 0.1 copy.11.port_ref
  36.3 1.0 %collective-permute-done.2.other_ref = f32[8,8,64]{2,1,0:T(8,128)S(1)} collective-permute-done((f32[8,8,64]{2,1,0:T(8,128)S(1)}, f32[8,8,64]{2,1,0:T(8,128)S(1)}, u32[]{:S(2)}, u32[]{:S(2)}) %collective-permute-start.2) | collective-permute-done | bytes 16416 | tf_op jit(solution)/shard_map/ppermute | solution.py:457
  37.4 0.1 coefficients.1
  37.5 0.0 copy-done.1
  37.5 2.2 %select_edges.5 = f32[64,3072]{1,0:T(8,128)S(1)} custom-call(f32[8,8,64]{2,1,0:T(8,128)S(1)} %get-tuple-element.10.refs_0_.coef_ref, s32[1,8192]{1,0:T(1,128)S(1)} %bitcast.9, f32[8,64,8192]{2,1,0:T(8,128)} %bitcast.15, f32[8,64,8192]{2,1,0:T(8,128)} %bitcast.16), custom_call_target="tpu_custom_call" | custom-call | tf_op jit(solution)/shard_map/select_edges/pallas_call | solution.py:378
  39.7 0.3 collective-permute-start.5
  40.0 1.1 %select_edges.4 = f32[64,1024]{1,0:T(8,128)S(1)} custom-call(f32[8,8,64]{2,1,0:T(8,128)S(1)} %get-tuple-element.10.refs_0_.coef_ref, s32[1,8192]{1,0:T(1,128)S(1)} %bitcast.10, f32[8,64,8192]{2,1,0:T(8,128)} %bitcast.17, f32[8,64,8192]{2,1,0:T(8,128)} %bitcast.18), custom_call_target="tpu_custom_call" | custom-call | tf_op jit(solution)/shard_map/select_edges/pallas_call | solution.py:378
  41.1 1.9 %collective-permute-start.4 = (f32[64,1024]{1,0:T(8,128)S(1)}, f32[64,1024]{1,0:T(8,128)S(1)}, u32[]{:S(2)}, u32[]{:S(2)}) collective-permute-start(f32[64,1024]{1,0:T(8,128)S(1)} %select_edges.4), channel_id=1, source_target_pairs={{0,2},{2,0},{1,3},{3,1},{4,6},{6,4},{5,7},{7,5},{8,10},{10,8},{9,1... | collective-permute-start | bytes 786440 | tf_op jit(solution)/shard_map/ppermute | solution.py:416
  43.0 0.2 collective-permute-start.3
  43.2 1.0 %select_edges.7 = f32[64,512]{1,0:T(8,128)S(1)} custom-call(s32[1,8192]{1,0:T(1,128)S(1)} %bitcast.11, f32[8,64,8192]{2,1,0:T(8,128)} %bitcast.19, f32[8,64,8192]{2,1,0:T(8,128)} %bitcast.20), custom_call_target="tpu_custom_call" | custom-call | tf_op jit(solution)/shard_map/select_edges/pallas_call | solution.py:378
  44.2 1.9 %collective-permute-start.7 = (f32[64,512]{1,0:T(8,128)S(1)}, f32[64,512]{1,0:T(8,128)S(1)}, u32[]{:S(2)}, u32[]{:S(2)}) collective-permute-start(f32[64,512]{1,0:T(8,128)S(1)} %select_edges.7), channel_id=1, source_target_pairs={{0,2},{2,0},{1,3},{3,1},{4,6},{6,4},{5,7},{7,5},{8,10},{10,8},{9,1... | collective-permute-start | bytes 393224 | tf_op jit(solution)/shard_map/ppermute | solution.py:416
  46.1 24.4 %slab_update.1.in_ref = f32[8,64,8192]{2,1,0:T(8,128)} custom-call(f32[8,8,64]{2,1,0:T(8,128)S(1)} %get-tuple-element.10.refs_0_.coef_ref, f32[8,2,128]{2,1,0:T(2,128)S(1)} %get-tuple-element.12.fac_ref, f32[8,8192]{1,0:T(8,128)S(1)} %get-tuple-element.11.rows_ref, f32[8,64,8192]{2,1,0:T(8,128)} %bitcast.21), custom_call_target="tpu_custom_call" | custom-call | tf_op jit(solution)/shard_map/slab_update/pallas_call | solution.py:275
  70.4 0.0 collective-permute-done.3
  70.4 0.0 collective-permute-done.7.halo_ref
  70.5 2.4 %edge_update.4.in_ref = f32[8,64,8192]{2,1,0:T(8,128)} custom-call(f32[8,64]{1,0:T(8,128)S(1)} %get-tuple-element.16.left_ref, f32[8,64]{1,0:T(8,128)S(1)} %get-tuple-element.15.right_ref, f32[8,8192]{1,0:T(8,128)S(1)} %get-tuple-element.11.rows_ref, f32[64,512]{1,0:T(8,128)S(1)} %collective-permute-done.7.halo_ref, ...), custom_call_target="tpu_custom_call", output_to_operand_aliasing={{}: (4, {})} | custom-call | tf_op jit(solution)/shard_map/edge_update/pallas_call | solution.py:344
  72.9 0.0 collective-permute-done.6.halo_ref
  72.9 12.8 %edge_update.5.in_ref = f32[8,64,8192]{2,1,0:T(8,128)} custom-call(f32[8,64]{1,0:T(8,128)S(1)} %get-tuple-element.16.left_ref, f32[8,64]{1,0:T(8,128)S(1)} %get-tuple-element.15.right_ref, f32[8,8192]{1,0:T(8,128)S(1)} %get-tuple-element.11.rows_ref, f32[64,3584]{1,0:T(8,128)S(1)} %collective-permute-done.6.halo_ref, ...), custom_call_target="tpu_custom_call", output_to_operand_aliasing={{}: (4, {})} | custom-call | tf_op jit(solution)/shard_map/edge_update/pallas_call | solution.py:344
  85.7 0.0 collective-permute-done.5.halo_ref
  85.7 7.9 %edge_update.6.in_ref = f32[8,64,8192]{2,1,0:T(8,128)} custom-call(f32[8,64]{1,0:T(8,128)S(1)} %get-tuple-element.16.left_ref, f32[8,64]{1,0:T(8,128)S(1)} %get-tuple-element.15.right_ref, f32[8,8192]{1,0:T(8,128)S(1)} %get-tuple-element.11.rows_ref, f32[64,3072]{1,0:T(8,128)S(1)} %collective-permute-done.5.halo_ref, ...), custom_call_target="tpu_custom_call", output_to_operand_aliasing={{}: (4, {})} | custom-call | tf_op jit(solution)/shard_map/edge_update/pallas_call | solution.py:344
  93.6 0.0 collective-permute-done.4.halo_ref
  93.6 3.1 %edge_update.7 = f32[8,64,8192]{2,1,0:T(8,128)} custom-call(f32[8,64]{1,0:T(8,128)S(1)} %get-tuple-element.16.left_ref, f32[8,64]{1,0:T(8,128)S(1)} %get-tuple-element.15.right_ref, f32[8,8192]{1,0:T(8,128)S(1)} %get-tuple-element.11.rows_ref, f32[64,1024]{1,0:T(8,128)S(1)} %collective-permute-done.4.halo_ref, ...), custom_call_target="tpu_custom_call", output_to_operand_aliasing={{}: (4, {})} | custom-call | tf_op jit(solution)/shard_map/edge_update/pallas_call | solution.py:344
  (5 shorter events, 0.0 us)
Async XLA Ops:
  0.0 0.8 copy-start
  4.9 31.3 %copy-start.2 = (s32[8,2]{0,1:T(2,128)S(1)}, s32[8,2]{0,1:T(2,128)}, u32[]{:S(2)}) copy-start(s32[8,2]{0,1:T(2,128)} %param.8) | copy-start | bytes 196
  4.9 31.4 %copy-start.3 = (s32[8,2]{0,1:T(2,128)S(1)}, s32[8,2]{0,1:T(2,128)}, u32[]{:S(2)}) copy-start(s32[8,2]{0,1:T(2,128)} %param.9) | copy-start | bytes 196
  4.9 32.6 %copy-start.1 = (s32[8192]{0:T(1024)S(1)}, s32[8192]{0:T(1024)}, u32[]{:S(2)}) copy-start(s32[8192]{0:T(1024)} %param.6) | copy-start | bytes 98308
  4.9 68.0 %collective-permute-start.6 = (f32[64,3584]{1,0:T(8,128)S(1)}, f32[64,3584]{1,0:T(8,128)S(1)}, u32[]{:S(2)}, u32[]{:S(2)}) collective-permute-start(f32[64,3584]{1,0:T(8,128)S(1)} %select_edges.6), channel_id=1, source_target_pairs={{0,2},{2,0},{1,3},{3,1},{4,6},{6,4},{5,7},{7,5},{8,10},{10,8},{9,1... | collective-permute-start | bytes 2752520 | tf_op jit(solution)/shard_map/ppermute | solution.py:416
  27.4 3.9 %collective-permute-start = (f32[8,8,64]{2,1,0:T(8,128)S(1)}, f32[8,8,64]{2,1,0:T(8,128)S(1)}, u32[]{:S(2)}, u32[]{:S(2)}) collective-permute-start(f32[8,8,64]{2,1,0:T(8,128)S(1)} %get-tuple-element.9), channel_id=1, source_target_pairs={{0,4},{4,0},{8,12},{12,8},{1,5},{5,1},{9,13},{13,9},{2,6},{6,2},{1... | collective-permute-start | bytes 49160 | tf_op jit(solution)/shard_map/ppermute | solution.py:434
  31.3 4.8 %collective-permute-start.1 = (f32[8,8,64]{2,1,0:T(8,128)S(1)}, f32[8,8,64]{2,1,0:T(8,128)S(1)}, u32[]{:S(2)}, u32[]{:S(2)}) collective-permute-start(f32[8,8,64]{2,1,0:T(8,128)S(1)} %add.6), channel_id=1, source_target_pairs={{0,8},{4,12},{8,0},{12,4},{1,9},{5,13},{9,1},{13,5},{2,10},{6,14},... | collective-permute-start | bytes 49160 | tf_op jit(solution)/shard_map/ppermute | solution.py:434
  36.2 1.2 %collective-permute-start.2 = (f32[8,8,64]{2,1,0:T(8,128)S(1)}, f32[8,8,64]{2,1,0:T(8,128)S(1)}, u32[]{:S(2)}, u32[]{:S(2)}) collective-permute-start(f32[8,8,64]{2,1,0:T(8,128)S(1)} %add.7.own_ref), channel_id=1, source_target_pairs={{0,1},{1,0},{2,3},{3,2},{4,5},{5,4},{6,7},{7,6},{8,9},{9,8},{10,11... | collective-permute-start | bytes 49160 | tf_op jit(solution)/shard_map/ppermute | solution.py:457
  39.7 46.0 %collective-permute-start.5 = (f32[64,3072]{1,0:T(8,128)S(1)}, f32[64,3072]{1,0:T(8,128)S(1)}, u32[]{:S(2)}, u32[]{:S(2)}) collective-permute-start(f32[64,3072]{1,0:T(8,128)S(1)} %select_edges.5), channel_id=1, source_target_pairs={{0,2},{2,0},{1,3},{3,1},{4,6},{6,4},{5,7},{7,5},{8,10},{10,8},{9,1... | collective-permute-start | bytes 2359304 | tf_op jit(solution)/shard_map/ppermute | solution.py:416
  41.1 52.6 %collective-permute-start.4 = (f32[64,1024]{1,0:T(8,128)S(1)}, f32[64,1024]{1,0:T(8,128)S(1)}, u32[]{:S(2)}, u32[]{:S(2)}) collective-permute-start(f32[64,1024]{1,0:T(8,128)S(1)} %select_edges.4), channel_id=1, source_target_pairs={{0,2},{2,0},{1,3},{3,1},{4,6},{6,4},{5,7},{7,5},{8,10},{10,8},{9,1... | collective-permute-start | bytes 786440 | tf_op jit(solution)/shard_map/ppermute | solution.py:416
  43.0 27.5 %collective-permute-start.3 = (f32[2,8,64]{2,1,0:T(8,128)S(1)}, f32[2,8,64]{2,1,0:T(8,128)S(1)}, u32[]{:S(2)}, u32[]{:S(2)}) collective-permute-start(f32[2,8,64]{2,1,0:T(8,128)S(1)} %pad_maximum_fusion), channel_id=1, source_target_pairs={{0,2},{2,0},{1,3},{3,1},{4,6},{6,4},{5,7},{7,5},{8,10},{10,8},{9,1... | collective-permute-start | bytes 12296 | tf_op jit(solution)/shard_map/ppermute | solution.py:423
  44.2 26.3 %collective-permute-start.7 = (f32[64,512]{1,0:T(8,128)S(1)}, f32[64,512]{1,0:T(8,128)S(1)}, u32[]{:S(2)}, u32[]{:S(2)}) collective-permute-start(f32[64,512]{1,0:T(8,128)S(1)} %select_edges.7), channel_id=1, source_target_pairs={{0,2},{2,0},{1,3},{3,1},{4,6},{6,4},{5,7},{7,5},{8,10},{10,8},{9,1... | collective-permute-start | bytes 393224 | tf_op jit(solution)/shard_map/ppermute | solution.py:416
